TPU v7x, 512 devices: a whole 4x8x8 slice. The times are simulated.
512 devices in a mesh: pipe: 2 (over core), tensor: 8 (over x, y_hi), expert: 32 (over y_lo, z).
Axes of the slice: x: 4, y: 8 (y_hi: 2, y_lo: 4; y = y_hi * 4 + y_lo), z: 8, core: 2. Of those that a mesh axis runs over, the one named last changes fastest.
Arguments:
- tokens: bfloat16 [3, 1536, 4096], P(None, 'expert', 'tensor'), may hold values from -36 to 36
- norm_gain: float32 [2, 4096], P('pipe'), may hold values from 0.1 to 1.9
- shared_gate: bfloat16 [2, 4096, 1024], P('pipe', 'expert', 'tensor'), may hold values from -0.09375 to 0.09375
- shared_up: bfloat16 [2, 4096, 1024], P('pipe', 'expert', 'tensor'), may hold values from -0.09375 to 0.09375
- shared_down: bfloat16 [2, 1024, 4096], P('pipe', 'tensor', 'expert'), may hold values from -0.1875 to 0.1875
- expert_gate: bfloat16 [2, 32, 4096, 1024], P('pipe', 'expert', None, 'tensor'), may hold values from -0.09375 to 0.09375
- expert_up: bfloat16 [2, 32, 4096, 1024], P('pipe', 'expert', None, 'tensor'), may hold values from -0.09375 to 0.09375
- expert_down: bfloat16 [2, 32, 1024, 4096], P('pipe', 'expert', 'tensor'), may hold values from -0.1875 to 0.1875
- expert_ids: int32 [2, 3, 1536, 8], P('pipe', None, 'expert'), may hold values from 0 to 255, as said below
- expert_slots: int32 [2, 3, 1536, 8], P('pipe', None, 'expert'), may hold values from -1 to 2, as said below
- route_weights: float32 [2, 3, 1536, 8], P('pipe', None, 'expert'), may hold values from 0.1 to 1
Outputs:
- states: bfloat16 [2, 3, 1536, 4096], P('pipe', None, 'expert', 'tensor')
Inputs may be any that keep to these rules, and one draw needn't show every extreme that they name: `expert_ids`: the 8 ids of a token are distinct. Ids of 32 and above name experts that are not held and add nothing. `expert_slots`: for a choice whose id is below 32: the number of earlier choices (earlier tokens, or lower k of the same token) of the same block of 48 tokens, same layer and microbatch, that name the same expert, if that number is below 3; otherwise -1. For ids of 32 and above: -1.
All inputs are finite; a program needn't handle non-finite values.
Results may differ from a plain program's by a relative error of at most 0.0085.
Values may be sent and summed in bfloat16 or wider, within the bound.
No kernel may reach another device: no remote copies, remote signals or barrier semaphores. Data moves between devices by JAX's collectives and lax.ppermute only.
A program may use at most 64 MiB of HBM per device.

v0:
```python
import jax
import jax.numpy as jnp
from jax import lax
from jax.sharding import PartitionSpec as P

CAP = 3


def turned_gather(arrays, axis, dims):
    turned = [jnp.moveaxis(a, dim, 0) for a, dim in zip(arrays, dims)]
    both = jnp.concatenate([t.reshape(len(t), -1) for t in turned], axis=1)
    filled, at, outs = (lax.all_gather(both, axis, axis=0, tiled=True), 0, [])
    for t, dim in zip(turned, dims):
        share = filled[:, at : at + t[0].size].reshape(-1, *t.shape[1:])
        outs.append(jnp.moveaxis(share, 0, dim))
        at += t[0].size
    return tuple(outs)


def laid_out(blocks, dim):
    shape = list(blocks.shape[1:])
    shape[dim] *= blocks.shape[0]
    return jnp.moveaxis(blocks, 0, dim).reshape(shape)


def from_everyone(x, axis):
    copies = jnp.broadcast_to(x, (lax.axis_size(axis), *x.shape))
    return lax.all_to_all(copies, axis, split_axis=0, concat_axis=0, tiled=True)


def gather_directly(x, axis, dim):
    return laid_out(from_everyone(x, axis), dim)


def in_blocks(x, dim, peers):
    shape = x.shape
    blocks = x.reshape(*shape[:dim], peers, shape[dim] // peers, *shape[dim + 1 :])
    return jnp.moveaxis(blocks, dim, 0)


def sent_and_summed(x, axis, dim):
    blocks = in_blocks(x, dim, lax.axis_size(axis))
    arrived = lax.all_to_all(blocks, axis, split_axis=0, concat_axis=0, tiled=True)
    return arrived.astype(jnp.float32).sum(axis=0)


def from_behind(value, axis, steps):
    count = lax.axis_size(axis)
    initial, last = (max(0, -steps), min(count, count - steps))
    return lax.ppermute(value, axis, [(source, source + steps) for source in range(initial, last)])


def product(left, right):
    return jnp.dot(left, right, preferred_element_type=jnp.float32)


def per_device(
    tokens,
    norm_gain,
    shared_gate,
    shared_up,
    shared_down,
    expert_gate,
    expert_up,
    expert_down,
    expert_ids,
    expert_slots,
    route_weights,
):
    section_index = lax.axis_index("pipe")
    n_experts = lax.axis_size("expert")
    n_tensor = lax.axis_size("tensor")
    batches = tokens.shape[0]
    shard_rows = tokens.shape[1]
    slice_width = tokens.shape[2]
    model_width = slice_width * n_tensor
    capacity = CAP
    slot_total = n_experts * capacity
    slot_range = jnp.arange(slot_total, dtype=jnp.int32)
    shared_gate_full, shared_up_full, shared_down_full = turned_gather(
        (shared_gate[0], shared_up[0], shared_down[0]), "expert", (0, 0, 1)
    )
    local_gate = expert_gate[0, 0]
    local_up = expert_up[0, 0]
    local_down = expert_down[0, 0]
    layer_gain = norm_gain[0]
    incoming = jnp.zeros((shard_rows, slice_width), jnp.bfloat16)
    produced = []
    for step_index in range(batches + 1):
        fresh_rows = tokens[min(step_index, batches - 1)]
        current = jnp.where(section_index == 0, fresh_rows, incoming)
        batch_index = jnp.clip(step_index - section_index, 0, batches - 1)
        route_ids = lax.dynamic_index_in_dim(expert_ids[0], batch_index, 0, keepdims=False)
        slot_rank = lax.dynamic_index_in_dim(expert_slots[0], batch_index, 0, keepdims=False)
        weights = lax.dynamic_index_in_dim(route_weights[0], batch_index, 0, keepdims=False)
        full_rows = gather_directly(current, "tensor", 1)
        values = full_rows.astype(jnp.float32)
        inverse_rms = lax.rsqrt(jnp.mean(values * values, axis=-1, keepdims=True) + 1e-06)
        normed = (values * inverse_rms * layer_gain).astype(jnp.bfloat16)
        shared_hidden = (
            jax.nn.silu(product(normed, shared_gate_full)) * product(normed, shared_up_full)
        ).astype(jnp.bfloat16)
        partial_value = product(shared_hidden, shared_down_full)
        valid = (route_ids < n_experts) & (slot_rank >= 0)
        slot_code = jnp.where(valid, route_ids * capacity + slot_rank, -1)
        matched = slot_code[:, :, None] == slot_range[None, None, :]
        picker = jnp.any(matched, axis=1).T.astype(jnp.bfloat16)
        combine = jnp.sum(jnp.where(matched, weights[:, :, None], jnp.float32(0.0)), axis=1)
        outgoing = (
            product(picker, normed).astype(jnp.bfloat16).reshape(n_experts, capacity, model_width)
        )
        arrived = lax.all_to_all(
            outgoing, "expert", split_axis=0, concat_axis=0, tiled=True
        ).reshape(slot_total, model_width)
        gate_rows = product(arrived, local_gate)
        up_rows = product(arrived, local_up)
        expert_hidden = (jax.nn.silu(gate_rows) * up_rows).astype(jnp.bfloat16)
        outcome = (
            product(expert_hidden, local_down)
            .astype(jnp.bfloat16)
            .reshape(n_experts, capacity, model_width)
        )
        returned = lax.all_to_all(
            outcome, "expert", split_axis=0, concat_axis=0, tiled=True
        ).reshape(slot_total, model_width)
        routed = jnp.dot(combine, returned.astype(jnp.float32), preferred_element_type=jnp.float32)
        summed = sent_and_summed((partial_value + routed).astype(jnp.bfloat16), "tensor", 1)
        result = (current.astype(jnp.float32) + summed).astype(jnp.bfloat16)
        produced.append(result)
        if step_index < batches:
            incoming = from_behind(result, "pipe", 1)
    outputs = [
        jnp.where(section_index == 0, produced[index_now], produced[index_now + 1])
        for index_now in range(batches)
    ]
    return jnp.stack(outputs)[None]


def solution(mesh):
    in_specs = (
        P(None, "expert", "tensor"),
        P("pipe", None),
        P("pipe", "expert", "tensor"),
        P("pipe", "expert", "tensor"),
        P("pipe", "tensor", "expert"),
        P("pipe", "expert", None, "tensor"),
        P("pipe", "expert", None, "tensor"),
        P("pipe", "expert", "tensor", None),
        P("pipe", None, "expert", None),
        P("pipe", None, "expert", None),
        P("pipe", None, "expert", None),
    )
    out_specs = P("pipe", None, "expert", "tensor")
    return jax.shard_map(
        per_device, mesh=mesh, in_specs=in_specs, out_specs=out_specs, check_vma=False
    )
```

profile of v0, /device:TPU:72, one launch (start us, length us, event | category | flops | bytes accessed | tf_op | source)
XLA Modules:
  0.0 615.7 jit_solution(16635909837770484328)
XLA Ops:
  8.2 8.7 %all-to-all-start = ((bf16[8,48,512]{2,1,0:T(8,128)(2,1)}), bf16[8,48,512]{2,1,0:T(8,128)(2,1)S(1)}, u32[]{:S(2)}, u32[]{:S(2)}) async-start(bf16[8,48,512]{2,1,0:T(8,128)(2,1)} %broadcast_in_dim.80), calls=%async_computation | async-start | bytes 786432 | tf_op jit(solution)/shard_map/all_to_all | solution.py:28
  21.8 11.9 %all-to-all-done = bf16[8,48,512]{2,1,0:T(8,128)(2,1)S(1)} async-done(((bf16[8,48,512]{2,1,0:T(8,128)(2,1)}), bf16[8,48,512]{2,1,0:T(8,128)(2,1)S(1)}, u32[]{:S(2)}, u32[]{:S(2)}) %all-to-all-start) | async-done | bytes 393248 | tf_op jit(solution)/shard_map/all_to_all | solution.py:28
  36.0 39.3 %all_to_all.80 = bf16[32,3,4096]{2,1,0:T(4,128)(2,1)} all-to-all(bf16[32,3,4096]{2,1,0:T(4,128)(2,1)} %reshape.259), channel_id=1, replica_groups=mesh['pipe'=2,'tensor'=8,'expert'=32] {'expert'}, dimensions={0} | all-to-all | bytes 1572864 | tf_op jit(solution)/shard_map/all_to_all | solution.py:112
  75.3 2.5 reshape.260
  79.8 2.7 convolution_convert_fusion.3
  82.6 2.3 reshape.261
  84.8 8.4 %all-to-all-start.2 = ((bf16[32,3,4096]{2,1,0:T(4,128)(2,1)}), bf16[32,3,4096]{2,1,0:T(4,128)(2,1)}, u32[]{:S(2)}, u32[]{:S(2)}) async-start(bf16[32,3,4096]{2,1,0:T(4,128)(2,1)} %reshape.261), calls=%async_computation.2 | async-start | bytes 2097152 | tf_op jit(solution)/shard_map/all_to_all | solution.py:123
  97.6 22.4 %all-to-all-done.2 = bf16[32,3,4096]{2,1,0:T(4,128)(2,1)} async-done(((bf16[32,3,4096]{2,1,0:T(4,128)(2,1)}), bf16[32,3,4096]{2,1,0:T(4,128)(2,1)}, u32[]{:S(2)}, u32[]{:S(2)}) %all-to-all-start.2) | async-done | bytes 786464 | tf_op jit(solution)/shard_map/all_to_all | solution.py:123
  120.0 2.5 reshape.262
  122.4 74.5 %all-gather.2.cloned.1.call-done = bf16[4096,384]{0,1:T(8,128)(2,1)} async-done(((bf16[128,384]{0,1:T(8,128)(2,1)}), bf16[4096,384]{0,1:T(8,128)(2,1)}) %all-gather.2.cloned.1.call-update) | async-done | bytes 3145744 | tf_op jit(solution)/shard_map/all_gather | solution.py:12
  196.9 2.3 fusion.58
  199.2 3.4 fusion.15
  204.3 17.6 %all_to_all.81 = bf16[8,48,512]{2,1,0:T(8,128)(2,1)S(1)} all-to-all(bf16[8,48,512]{2,1,0:T(8,128)(2,1)S(1)} %bitcast.150), channel_id=1, replica_groups=mesh['pipe'=2,'tensor'=8,'expert'=32] {'tensor'}, dimensions={0} | all-to-all | bytes 786432 | tf_op jit(solution)/shard_map/all_to_all | solution.py:43
  225.6 3.5 all-to-all-start.4
  231.9 12.8 %all-to-all-done.4 = bf16[8,48,512]{2,1,0:T(8,128)(2,1)S(1)} async-done(((bf16[8,48,512]{2,1,0:T(8,128)(2,1)}), bf16[8,48,512]{2,1,0:T(8,128)(2,1)S(1)}, u32[]{:S(2)}, u32[]{:S(2)}) %all-to-all-start.4) | async-done | bytes 393248 | tf_op jit(solution)/shard_map/all_to_all | solution.py:28
  246.7 2.3 reshape.264
  248.9 39.0 %all_to_all.82 = bf16[32,3,4096]{2,1,0:T(4,128)(2,1)} all-to-all(bf16[32,3,4096]{2,1,0:T(4,128)(2,1)} %reshape.264), channel_id=1, replica_groups=mesh['pipe'=2,'tensor'=8,'expert'=32] {'expert'}, dimensions={0} | all-to-all | bytes 1572864 | tf_op jit(solution)/shard_map/all_to_all | solution.py:112
  288.0 2.5 reshape.265
  292.5 2.8 convolution_convert_fusion.2
  295.3 2.3 reshape.266
  297.6 5.5 all-to-all-start.6
  306.0 2.3 fusion.56
  308.3 3.4 fusion.14
  311.7 19.5 %all-to-all-done.6 = bf16[32,3,4096]{2,1,0:T(4,128)(2,1)} async-done(((bf16[32,3,4096]{2,1,0:T(4,128)(2,1)}), bf16[32,3,4096]{2,1,0:T(4,128)(2,1)}, u32[]{:S(2)}, u32[]{:S(2)}) %all-to-all-start.6) | async-done | bytes 786464 | tf_op jit(solution)/shard_map/all_to_all | solution.py:123
  331.2 2.5 reshape.267
  335.3 20.7 %all_to_all.83 = bf16[8,48,512]{2,1,0:T(8,128)(2,1)S(1)} all-to-all(bf16[8,48,512]{2,1,0:T(8,128)(2,1)S(1)} %bitcast.151), channel_id=1, replica_groups=mesh['pipe'=2,'tensor'=8,'expert'=32] {'tensor'}, dimensions={0} | all-to-all | bytes 786432 | tf_op jit(solution)/shard_map/all_to_all | solution.py:43
  361.1 3.6 all-to-all-start.8
  367.6 12.8 %all-to-all-done.8 = bf16[8,48,512]{2,1,0:T(8,128)(2,1)S(1)} async-done(((bf16[8,48,512]{2,1,0:T(8,128)(2,1)}), bf16[8,48,512]{2,1,0:T(8,128)(2,1)S(1)}, u32[]{:S(2)}, u32[]{:S(2)}) %all-to-all-start.8) | async-done | bytes 393248 | tf_op jit(solution)/shard_map/all_to_all | solution.py:28
  382.3 2.3 reshape.269
  384.6 33.6 %all_to_all.84 = bf16[32,3,4096]{2,1,0:T(4,128)(2,1)} all-to-all(bf16[32,3,4096]{2,1,0:T(4,128)(2,1)} %reshape.269), channel_id=1, replica_groups=mesh['pipe'=2,'tensor'=8,'expert'=32] {'expert'}, dimensions={0} | all-to-all | bytes 1572864 | tf_op jit(solution)/shard_map/all_to_all | solution.py:112
  418.2 2.5 reshape.270
  422.7 2.8 convolution_convert_fusion.1
  425.5 2.3 reshape.271
  427.8 5.4 all-to-all-start.10
  436.0 2.3 fusion.54
  438.3 3.4 fusion.13
  441.8 19.5 %all-to-all-done.10 = bf16[32,3,4096]{2,1,0:T(4,128)(2,1)} async-done(((bf16[32,3,4096]{2,1,0:T(4,128)(2,1)}), bf16[32,3,4096]{2,1,0:T(4,128)(2,1)}, u32[]{:S(2)}, u32[]{:S(2)}) %all-to-all-start.10) | async-done | bytes 786464 | tf_op jit(solution)/shard_map/all_to_all | solution.py:123
  461.2 2.5 reshape.272
  465.4 17.9 %all_to_all.85 = bf16[8,48,512]{2,1,0:T(8,128)(2,1)S(1)} all-to-all(bf16[8,48,512]{2,1,0:T(8,128)(2,1)S(1)} %bitcast.152), channel_id=1, replica_groups=mesh['pipe'=2,'tensor'=8,'expert'=32] {'tensor'}, dimensions={0} | all-to-all | bytes 786432 | tf_op jit(solution)/shard_map/all_to_all | solution.py:43
  488.4 3.5 all-to-all-start.12
  494.7 12.9 %all-to-all-done.12 = bf16[8,48,512]{2,1,0:T(8,128)(2,1)S(1)} async-done(((bf16[8,48,512]{2,1,0:T(8,128)(2,1)}), bf16[8,48,512]{2,1,0:T(8,128)(2,1)S(1)}, u32[]{:S(2)}, u32[]{:S(2)}) %all-to-all-start.12) | async-done | bytes 393248 | tf_op jit(solution)/shard_map/all_to_all | solution.py:28
  509.6 2.3 reshape.274
  511.8 35.0 %all_to_all.86 = bf16[32,3,4096]{2,1,0:T(4,128)(2,1)} all-to-all(bf16[32,3,4096]{2,1,0:T(4,128)(2,1)} %reshape.274), channel_id=1, replica_groups=mesh['pipe'=2,'tensor'=8,'expert'=32] {'expert'}, dimensions={0} | all-to-all | bytes 1572864 | tf_op jit(solution)/shard_map/all_to_all | solution.py:112
  546.8 2.5 reshape.275
  554.5 5.4 all-to-all-start.14
  561.9 3.3 fusion.12
  565.3 22.7 %all-to-all-done.14 = bf16[32,3,4096]{2,1,0:T(4,128)(2,1)S(1)} async-done(((bf16[32,3,4096]{2,1,0:T(4,128)(2,1)}), bf16[32,3,4096]{2,1,0:T(4,128)(2,1)S(1)}, u32[]{:S(2)}, u32[]{:S(2)}) %all-to-all-start.14) | async-done | bytes 786464 | tf_op jit(solution)/shard_map/all_to_all | solution.py:123
  590.1 17.9 %all_to_all.87 = bf16[8,48,512]{2,1,0:T(8,128)(2,1)S(1)} all-to-all(bf16[8,48,512]{2,1,0:T(8,128)(2,1)S(1)} %bitcast.153), channel_id=1, replica_groups=mesh['pipe'=2,'tensor'=8,'expert'=32] {'tensor'}, dimensions={0} | all-to-all | bytes 786432 | tf_op jit(solution)/shard_map/all_to_all | solution.py:43
  (137 shorter events, 68.4 us)
Async XLA Ops:
  6.5 73.3 %copy-start = (bf16[1,1,128,4096]{3,2,1,0:T(8,128)(2,1)S(1)}, bf16[1,1,128,4096]{3,2,1,0:T(8,128)(2,1)}, u32[]{:S(2)}) copy-start(bf16[1,1,128,4096]{3,2,1,0:T(8,128)(2,1)} %param.18) | copy-start | bytes 3145732
  6.5 27.5 %copy-start.10 = (f32[1,4096]{1,0:T(1,128)S(1)}, f32[1,4096]{1,0:T(1,128)}, u32[]{:S(2)}) copy-start(f32[1,4096]{1,0:T(1,128)} %param.12) | copy-start | bytes 49156
  8.2 25.5 %all-to-all-start = ((bf16[8,48,512]{2,1,0:T(8,128)(2,1)}), bf16[8,48,512]{2,1,0:T(8,128)(2,1)S(1)}, u32[]{:S(2)}, u32[]{:S(2)}) async-start(bf16[8,48,512]{2,1,0:T(8,128)(2,1)} %broadcast_in_dim.80), calls=%async_computation | async-start | bytes 786432 | tf_op jit(solution)/shard_map/all_to_all | solution.py:28
  16.9 180.0 %all-gather.2.cloned.1.call-start = ((), (), s32[]{:S(2)}) async-start(), calls=%async_computation.16 | async-start | bytes 3244032 | tf_op jit(solution)/shard_map/all_gather | solution.py:12
  21.6 12.4 %copy-start.11 = (s32[48,8]{1,0:T(8,128)}, s32[48,8]{1,0:T(8,128)S(1)}, u32[]{:S(2)}) copy-start(s32[48,8]{1,0:T(8,128)S(1)} %copy.49) | copy-start | bytes 4612
  34.6 43.1 %copy-start.2 = (bf16[1,1,4096,128]{3,2,1,0:T(8,128)(2,1)S(1)}, bf16[1,1,4096,128]{3,2,1,0:T(8,128)(2,1)}, u32[]{:S(2)}) copy-start(bf16[1,1,4096,128]{3,2,1,0:T(8,128)(2,1)} %param.16) | copy-start | bytes 3145732
  35.9 43.9 %copy-start.1 = (bf16[1,1,4096,128]{3,2,1,0:T(8,128)(2,1)S(1)}, bf16[1,1,4096,128]{3,2,1,0:T(8,128)(2,1)}, u32[]{:S(2)}) copy-start(bf16[1,1,4096,128]{3,2,1,0:T(8,128)(2,1)} %param.17) | copy-start | bytes 3145732
  84.8 35.1 %all-to-all-start.2 = ((bf16[32,3,4096]{2,1,0:T(4,128)(2,1)}), bf16[32,3,4096]{2,1,0:T(4,128)(2,1)}, u32[]{:S(2)}, u32[]{:S(2)}) async-start(bf16[32,3,4096]{2,1,0:T(4,128)(2,1)} %reshape.261), calls=%async_computation.2 | async-start | bytes 2097152 | tf_op jit(solution)/shard_map/all_to_all | solution.py:123
  202.5 19.4 %copy-start.9 = (bf16[3,48,512]{2,1,0:T(8,128)(2,1)S(1)}, bf16[3,48,512]{2,1,0:T(8,128)(2,1)}, u32[]{:S(2)}) copy-start(bf16[3,48,512]{2,1,0:T(8,128)(2,1)} %param.11) | copy-start | bytes 442372
  222.0 2.2 copy-start.17
  222.0 2.2 collective-permute-start
  224.2 0.6 copy-start.3
  225.6 19.1 %all-to-all-start.4 = ((bf16[8,48,512]{2,1,0:T(8,128)(2,1)}), bf16[8,48,512]{2,1,0:T(8,128)(2,1)S(1)}, u32[]{:S(2)}, u32[]{:S(2)}) async-start(bf16[8,48,512]{2,1,0:T(8,128)(2,1)} %broadcast_in_dim.85), calls=%async_computation.4 | async-start | bytes 786432 | tf_op jit(solution)/shard_map/all_to_all | solution.py:28
  244.7 0.7 copy-start.21
  297.6 33.6 %all-to-all-start.6 = ((bf16[32,3,4096]{2,1,0:T(4,128)(2,1)}), bf16[32,3,4096]{2,1,0:T(4,128)(2,1)}, u32[]{:S(2)}, u32[]{:S(2)}) async-start(bf16[32,3,4096]{2,1,0:T(4,128)(2,1)} %reshape.266), calls=%async_computation.6 | async-start | bytes 2097152 | tf_op jit(solution)/shard_map/all_to_all | solution.py:123
  311.7 44.4 %copy-start.4 = (bf16[48,512]{1,0:T(8,128)(2,1)S(1)}, bf16[48,512]{1,0:T(8,128)(2,1)}, u32[]{:S(2)}) copy-start(bf16[48,512]{1,0:T(8,128)(2,1)} %copy-done.3) | copy-start | bytes 147460
  311.7 44.4 %copy-start.18 = (bf16[48,512]{1,0:T(8,128)(2,1)S(1)}, bf16[48,512]{1,0:T(8,128)(2,1)}, u32[]{:S(2)}) copy-start(bf16[48,512]{1,0:T(8,128)(2,1)} %copy-done.17) | copy-start | bytes 147460
  356.7 4.4 copy-start.15
  356.7 2.1 collective-permute-start.1
  359.7 0.6 copy-start.5
  361.1 19.3 %all-to-all-start.8 = ((bf16[8,48,512]{2,1,0:T(8,128)(2,1)}), bf16[8,48,512]{2,1,0:T(8,128)(2,1)S(1)}, u32[]{:S(2)}, u32[]{:S(2)}) async-start(bf16[8,48,512]{2,1,0:T(8,128)(2,1)} %broadcast_in_dim.88), calls=%async_computation.8 | async-start | bytes 786432 | tf_op jit(solution)/shard_map/all_to_all | solution.py:28
  380.3 0.7 copy-start.22
  427.8 33.4 %all-to-all-start.10 = ((bf16[32,3,4096]{2,1,0:T(4,128)(2,1)}), bf16[32,3,4096]{2,1,0:T(4,128)(2,1)}, u32[]{:S(2)}, u32[]{:S(2)}) async-start(bf16[32,3,4096]{2,1,0:T(4,128)(2,1)} %reshape.271), calls=%async_computation.10 | async-start | bytes 2097152 | tf_op jit(solution)/shard_map/all_to_all | solution.py:123
  441.8 41.6 %copy-start.6 = (bf16[48,512]{1,0:T(8,128)(2,1)S(1)}, bf16[48,512]{1,0:T(8,128)(2,1)}, u32[]{:S(2)}) copy-start(bf16[48,512]{1,0:T(8,128)(2,1)} %copy-done.5) | copy-start | bytes 147460
  441.8 41.6 %copy-start.16 = (bf16[48,512]{1,0:T(8,128)(2,1)S(1)}, bf16[48,512]{1,0:T(8,128)(2,1)}, u32[]{:S(2)}) copy-start(bf16[48,512]{1,0:T(8,128)(2,1)} %copy-done.15) | copy-start | bytes 147460
  484.0 4.4 copy-start.19
  484.0 2.1 collective-permute-start.2
  487.0 0.6 copy-start.7
  488.4 19.2 %all-to-all-start.12 = ((bf16[8,48,512]{2,1,0:T(8,128)(2,1)}), bf16[8,48,512]{2,1,0:T(8,128)(2,1)S(1)}, u32[]{:S(2)}, u32[]{:S(2)}) async-start(bf16[8,48,512]{2,1,0:T(8,128)(2,1)} %broadcast_in_dim.91), calls=%async_computation.12 | async-start | bytes 786432 | tf_op jit(solution)/shard_map/all_to_all | solution.py:28
  507.6 0.7 copy-start.23
  551.4 8.6 %copy-start.24 = (f32[48,8]{0,1:T(8,128)S(1)}, f32[48,8]{0,1:T(8,128)}, u32[]{:S(2)}) copy-start(f32[48,8]{0,1:T(8,128)} %get-tuple-element.13) | copy-start | bytes 4612
  551.4 8.6 %copy-start.12 = (s32[48,8]{1,0:T(8,128)S(1)}, s32[48,8]{1,0:T(8,128)}, u32[]{:S(2)}) copy-start(s32[48,8]{1,0:T(8,128)} %copy.61) | copy-start | bytes 4612
  554.5 33.5 %all-to-all-start.14 = ((bf16[32,3,4096]{2,1,0:T(4,128)(2,1)}), bf16[32,3,4096]{2,1,0:T(4,128)(2,1)S(1)}, u32[]{:S(2)}, u32[]{:S(2)}) async-start(bf16[32,3,4096]{2,1,0:T(4,128)(2,1)} %reshape.276), calls=%async_computation.14 | async-start | bytes 2097152 | tf_op jit(solution)/shard_map/all_to_all | solution.py:123
  565.3 42.8 %copy-start.8 = (bf16[48,512]{1,0:T(8,128)(2,1)S(1)}, bf16[48,512]{1,0:T(8,128)(2,1)}, u32[]{:S(2)}) copy-start(bf16[48,512]{1,0:T(8,128)(2,1)} %copy-done.7) | copy-start | bytes 147460
  565.3 42.8 %copy-start.20 = (bf16[48,512]{1,0:T(8,128)(2,1)S(1)}, bf16[48,512]{1,0:T(8,128)(2,1)}, u32[]{:S(2)}) copy-start(bf16[48,512]{1,0:T(8,128)(2,1)} %copy-done.19) | copy-start | bytes 147460
  565.3 42.9 %copy-start.13 = (bf16[1,48,512]{2,1,0:T(8,128)(2,1)S(1)}, bf16[1,48,512]{2,1,0:T(8,128)(2,1)}, u32[]{:S(2)}) copy-start(bf16[1,48,512]{2,1,0:T(8,128)(2,1)} %get-tuple-element.5) | copy-start | bytes 147460
  565.3 42.9 %copy-start.14 = (bf16[1,48,512]{2,1,0:T(8,128)(2,1)S(1)}, bf16[1,48,512]{2,1,0:T(8,128)(2,1)}, u32[]{:S(2)}) copy-start(bf16[1,48,512]{2,1,0:T(8,128)(2,1)} %get-tuple-element.7) | copy-start | bytes 147460
Sparse Core Ops, SparseCore 0:
  20.2 176.5 all-gather.1
where the time goes:
time: 619 us; the launch traced here: 616 us
  blocking collectives  221 us (36%)
  waiting for transfers between devices  212 us (34%)
  local copies, waits for them, and re-layouts  51.6 us (8%)
  matrix products  51.2 us (8%)
  starting transfers between devices  47.8 us (8%)
  other arithmetic  18.6 us (3%)
  between operations  13.9 us (2%)
    all_to_all x4, blocking collectives, per_device(): lax.all_to_all(outgoing, 'expert', split_axis=0, concat_axis=0, tiled=True)  147 us
    all_to_all x4, waiting for transfers between devices, per_device(): lax.all_to_all(outcome, 'expert', split_axis=0, concat_axis=0, tiled=True)  84.1 us
    all_gather x1, waiting for transfers between devices, turned_gather(): filled, at, outs = (lax.all_gather(both, axis, axis=0, tiled=True), 0, [])  74.5 us
    all_to_all x4, blocking collectives, sent_and_summed(): lax.all_to_all(blocks, axis, split_axis=0, concat_axis=0, tiled=True)  74.1 us
    all_to_all x4, waiting for transfers between devices, from_everyone(): return lax.all_to_all(copies, axis, split_axis=0, concat_axis=0, tiled=True)  50.4 us
    dot_general x20, matrix products, product(): return jnp.dot(left, right, preferred_element_type=jnp.float32)  44.9 us
    all_to_all x4, starting transfers between devices, per_device(): lax.all_to_all(outcome, 'expert', split_axis=0, concat_axis=0, tiled=True)  24.7 us
    all_to_all x4, starting transfers between devices, from_everyone(): return lax.all_to_all(copies, axis, split_axis=0, concat_axis=0, tiled=True)  19.2 us
  transfers between devices with their start and end apart: 12, of which 12 were waited for; matrix products, arithmetic and copies ran while one was open for 9% of the time, Pallas kernels for 0%

commit v1 on v0

--- a/solution.py
+++ b/solution.py
@@ -9,7 +9,13 @@
 def turned_gather(arrays, axis, dims):
     turned = [jnp.moveaxis(a, dim, 0) for a, dim in zip(arrays, dims)]
     both = jnp.concatenate([t.reshape(len(t), -1) for t in turned], axis=1)
-    filled, at, outs = (lax.all_gather(both, axis, axis=0, tiled=True), 0, [])
+    filled, at, outs = (
+        jnp.concatenate(
+            lax.all_to_all(jnp.stack([both] * lax.axis_size(axis)), axis, 0, 0), axis=0
+        ),
+        0,
+        [],
+    )
     for t, dim in zip(turned, dims):
         share = filled[:, at : at + t[0].size].reshape(-1, *t.shape[1:])
         outs.append(jnp.moveaxis(share, 0, dim))

time: 619 us -> 646 us (1.044)
  blocking collectives: 221 us -> 253 us
  between operations: 13.9 us -> 0.48 us
    all_to_all x0 -> x1, waiting for transfers between devices: none -> 75.6 us  [turned_gather(): lax.all_to_all(jnp.stack([both] * lax.axis_size(axis)), axis, 0, 0)]
    all_gather x1 -> x0, waiting for transfers between devices: 74.5 us -> none  [turned_gather(): filled, at, outs = (lax.all_gather(both, axis, axis=0, tiled=True), 0, [])]
    all_to_all x4, blocking collectives: 74.1 us -> 105 us  [sent_and_summed(): lax.all_to_all(blocks, axis, split_axis=0, concat_axis=0, tiled=True)]
  transfers between devices with their start and end apart: 12 -> 12, of which waited for: 12 -> 12; matrix products, arithmetic and copies ran while one was open for 9% -> 7% of each run, Pallas kernels for 0% -> 0%
where the time goes in v1:
time: 646 us; the launch traced here: 643 us
  blocking collectives  253 us (39%)
  waiting for transfers between devices  214 us (33%)
  local copies, waits for them, and re-layouts  57.5 us (9%)
  matrix products  49.7 us (8%)
  starting transfers between devices  49.2 us (8%)
  other arithmetic  18.7 us (3%)
    all_to_all x4, blocking collectives, per_device(): lax.all_to_all(outgoing, 'expert', split_axis=0, concat_axis=0, tiled=True)  148 us
    all_to_all x4, blocking collectives, sent_and_summed(): lax.all_to_all(blocks, axis, split_axis=0, concat_axis=0, tiled=True)  105 us
    all_to_all x4, waiting for transfers between devices, per_device(): lax.all_to_all(outcome, 'expert', split_axis=0, concat_axis=0, tiled=True)  84.8 us
    all_to_all x1, waiting for transfers between devices, turned_gather(): lax.all_to_all(jnp.stack([both] * lax.axis_size(axis)), axis, 0, 0)  75.6 us
    all_to_all x4, waiting for transfers between devices, from_everyone(): return lax.all_to_all(copies, axis, split_axis=0, concat_axis=0, tiled=True)  51.1 us
    dot_general x20, matrix products, product(): return jnp.dot(left, right, preferred_element_type=jnp.float32)  43.4 us
    all_to_all x4, starting transfers between devices, per_device(): lax.all_to_all(outcome, 'expert', split_axis=0, concat_axis=0, tiled=True)  21 us
    all_to_all x4, starting transfers between devices, from_everyone(): return lax.all_to_all(copies, axis, split_axis=0, concat_axis=0, tiled=True)  19 us
  transfers between devices with their start and end apart: 12, of which 12 were waited for; matrix products, arithmetic and copies ran while one was open for 7% of the time, Pallas kernels for 0%

profile of v1, /device:TPU:72, one launch (start us, length us, event | category | flops | bytes accessed | tf_op | source)
XLA Modules:
  0.0 642.5 jit_solution(14029251951786205473)
XLA Ops:
  1.7 8.7 %all-to-all-start = ((bf16[8,48,512]{2,1,0:T(8,128)(2,1)}), bf16[8,48,512]{2,1,0:T(8,128)(2,1)S(1)}, u32[]{:S(2)}, u32[]{:S(2)}) async-start(bf16[8,48,512]{2,1,0:T(8,128)(2,1)} %broadcast_in_dim.80), calls=%async_computation | async-start | bytes 786432 | tf_op jit(solution)/shard_map/all_to_all | solution.py:34
  12.0 15.2 %all-to-all-done = bf16[8,48,512]{2,1,0:T(8,128)(2,1)S(1)} async-done(((bf16[8,48,512]{2,1,0:T(8,128)(2,1)}), bf16[8,48,512]{2,1,0:T(8,128)(2,1)S(1)}, u32[]{:S(2)}, u32[]{:S(2)}) %all-to-all-start) | async-done | bytes 393248 | tf_op jit(solution)/shard_map/all_to_all | solution.py:34
  29.4 39.2 %all_to_all.85 = bf16[32,3,4096]{2,1,0:T(4,128)(2,1)} all-to-all(bf16[32,3,4096]{2,1,0:T(4,128)(2,1)} %reshape.265), channel_id=1, replica_groups=mesh['pipe'=2,'tensor'=8,'expert'=32] {'expert'}, dimensions={0} | all-to-all | bytes 1572864 | tf_op jit(solution)/shard_map/all_to_all | solution.py:118
  68.6 2.5 reshape.266
  73.2 2.7 convolution_convert_fusion.3
  75.9 2.3 reshape.267
  78.2 5.4 all-to-all-start.3
  89.6 22.2 %all-to-all-done.3 = bf16[32,3,4096]{2,1,0:T(4,128)(2,1)} async-done(((bf16[32,3,4096]{2,1,0:T(4,128)(2,1)}), bf16[32,3,4096]{2,1,0:T(4,128)(2,1)}, u32[]{:S(2)}, u32[]{:S(2)}) %all-to-all-start.3) | async-done | bytes 786464 | tf_op jit(solution)/shard_map/all_to_all | solution.py:129
  111.8 3.0 stack.10
  114.8 5.3 all-to-all-start.1
  124.4 2.5 reshape.268
  126.9 75.6 %all-to-all-done.1 = bf16[32,128,384]{2,1,0:T(8,128)(2,1)} async-done(((bf16[32,128,384]{2,1,0:T(8,128)(2,1)}), bf16[32,128,384]{2,1,0:T(8,128)(2,1)}, u32[]{:S(2)}, u32[]{:S(2)}) %all-to-all-start.1) | async-done | bytes 3145760 | tf_op jit(solution)/shard_map/all_to_all | solution.py:14
  204.7 3.1 fusion.15
  209.5 51.1 %all_to_all.86 = bf16[8,48,512]{2,1,0:T(8,128)(2,1)S(1)} all-to-all(bf16[8,48,512]{2,1,0:T(8,128)(2,1)S(1)} %bitcast.151), channel_id=1, replica_groups=mesh['pipe'=2,'tensor'=8,'expert'=32] {'tensor'}, dimensions={0} | all-to-all | bytes 786432 | tf_op jit(solution)/shard_map/all_to_all | solution.py:49
  264.3 3.5 all-to-all-start.5
  270.6 10.5 %all-to-all-done.5 = bf16[8,48,512]{2,1,0:T(8,128)(2,1)S(1)} async-done(((bf16[8,48,512]{2,1,0:T(8,128)(2,1)}), bf16[8,48,512]{2,1,0:T(8,128)(2,1)S(1)}, u32[]{:S(2)}, u32[]{:S(2)}) %all-to-all-start.5) | async-done | bytes 393248 | tf_op jit(solution)/shard_map/all_to_all | solution.py:34
  283.1 2.3 reshape.270
  285.3 38.2 %all_to_all.87 = bf16[32,3,4096]{2,1,0:T(4,128)(2,1)} all-to-all(bf16[32,3,4096]{2,1,0:T(4,128)(2,1)} %reshape.270), channel_id=1, replica_groups=mesh['pipe'=2,'tensor'=8,'expert'=32] {'expert'}, dimensions={0} | all-to-all | bytes 1572864 | tf_op jit(solution)/shard_map/all_to_all | solution.py:118
  323.5 2.5 reshape.271
  328.1 2.7 convolution_convert_fusion.2
  330.8 2.3 reshape.272
  333.1 4.6 all-to-all-start.7
  342.7 3.2 fusion.14
  345.9 19.7 %all-to-all-done.7 = bf16[32,3,4096]{2,1,0:T(4,128)(2,1)} async-done(((bf16[32,3,4096]{2,1,0:T(4,128)(2,1)}), bf16[32,3,4096]{2,1,0:T(4,128)(2,1)}, u32[]{:S(2)}, u32[]{:S(2)}) %all-to-all-start.7) | async-done | bytes 786464 | tf_op jit(solution)/shard_map/all_to_all | solution.py:129
  365.6 2.5 reshape.273
  369.7 18.5 %all_to_all.88 = bf16[8,48,512]{2,1,0:T(8,128)(2,1)S(1)} all-to-all(bf16[8,48,512]{2,1,0:T(8,128)(2,1)S(1)} %bitcast.152), channel_id=1, replica_groups=mesh['pipe'=2,'tensor'=8,'expert'=32] {'tensor'}, dimensions={0} | all-to-all | bytes 786432 | tf_op jit(solution)/shard_map/all_to_all | solution.py:49
  393.3 3.5 all-to-all-start.9
  399.6 12.6 %all-to-all-done.9 = bf16[8,48,512]{2,1,0:T(8,128)(2,1)S(1)} async-done(((bf16[8,48,512]{2,1,0:T(8,128)(2,1)}), bf16[8,48,512]{2,1,0:T(8,128)(2,1)S(1)}, u32[]{:S(2)}, u32[]{:S(2)}) %all-to-all-start.9) | async-done | bytes 393248 | tf_op jit(solution)/shard_map/all_to_all | solution.py:34
  414.2 2.3 reshape.275
  416.5 35.1 %all_to_all.89 = bf16[32,3,4096]{2,1,0:T(4,128)(2,1)} all-to-all(bf16[32,3,4096]{2,1,0:T(4,128)(2,1)} %reshape.275), channel_id=1, replica_groups=mesh['pipe'=2,'tensor'=8,'expert'=32] {'expert'}, dimensions={0} | all-to-all | bytes 1572864 | tf_op jit(solution)/shard_map/all_to_all | solution.py:118
  451.5 2.5 reshape.276
  456.1 2.7 convolution_convert_fusion.1
  458.8 2.3 reshape.277
  461.1 5.6 all-to-all-start.11
  469.6 2.1 fusion.54
  471.8 3.2 fusion.13
  475.0 19.9 %all-to-all-done.11 = bf16[32,3,4096]{2,1,0:T(4,128)(2,1)} async-done(((bf16[32,3,4096]{2,1,0:T(4,128)(2,1)}), bf16[32,3,4096]{2,1,0:T(4,128)(2,1)}, u32[]{:S(2)}, u32[]{:S(2)}) %all-to-all-start.11) | async-done | bytes 786464 | tf_op jit(solution)/shard_map/all_to_all | solution.py:129
  494.8 2.5 reshape.278
  499.0 17.9 %all_to_all.90 = bf16[8,48,512]{2,1,0:T(8,128)(2,1)S(1)} all-to-all(bf16[8,48,512]{2,1,0:T(8,128)(2,1)S(1)} %bitcast.153), channel_id=1, replica_groups=mesh['pipe'=2,'tensor'=8,'expert'=32] {'tensor'}, dimensions={0} | all-to-all | bytes 786432 | tf_op jit(solution)/shard_map/all_to_all | solution.py:49
  521.9 3.5 all-to-all-start.13
  528.2 12.9 %all-to-all-done.13 = bf16[8,48,512]{2,1,0:T(8,128)(2,1)S(1)} async-done(((bf16[8,48,512]{2,1,0:T(8,128)(2,1)}), bf16[8,48,512]{2,1,0:T(8,128)(2,1)S(1)}, u32[]{:S(2)}, u32[]{:S(2)}) %all-to-all-start.13) | async-done | bytes 393248 | tf_op jit(solution)/shard_map/all_to_all | solution.py:34
  543.1 2.3 reshape.280
  545.4 35.1 %all_to_all.91 = bf16[32,3,4096]{2,1,0:T(4,128)(2,1)} all-to-all(bf16[32,3,4096]{2,1,0:T(4,128)(2,1)} %reshape.280), channel_id=1, replica_groups=mesh['pipe'=2,'tensor'=8,'expert'=32] {'expert'}, dimensions={0} | all-to-all | bytes 1572864 | tf_op jit(solution)/shard_map/all_to_all | solution.py:118
  580.5 2.5 reshape.281
  588.2 5.4 all-to-all-start.15
  595.4 3.2 fusion.12
  598.6 23.1 %all-to-all-done.15 = bf16[32,3,4096]{2,1,0:T(4,128)(2,1)S(1)} async-done(((bf16[32,3,4096]{2,1,0:T(4,128)(2,1)}), bf16[32,3,4096]{2,1,0:T(4,128)(2,1)S(1)}, u32[]{:S(2)}, u32[]{:S(2)}) %all-to-all-start.15) | async-done | bytes 786464 | tf_op jit(solution)/shard_map/all_to_all | solution.py:129
  623.9 17.9 %all_to_all.92 = bf16[8,48,512]{2,1,0:T(8,128)(2,1)S(1)} all-to-all(bf16[8,48,512]{2,1,0:T(8,128)(2,1)S(1)} %bitcast.154), channel_id=1, replica_groups=mesh['pipe'=2,'tensor'=8,'expert'=32] {'tensor'}, dimensions={0} | all-to-all | bytes 786432 | tf_op jit(solution)/shard_map/all_to_all | solution.py:49
  (138 shorter events, 75.3 us)
Async XLA Ops:
  0.0 73.2 %copy-start = (bf16[1,1,128,4096]{3,2,1,0:T(8,128)(2,1)S(1)}, bf16[1,1,128,4096]{3,2,1,0:T(8,128)(2,1)}, u32[]{:S(2)}) copy-start(bf16[1,1,128,4096]{3,2,1,0:T(8,128)(2,1)} %param.18) | copy-start | bytes 3145732
  0.0 27.5 %copy-start.10 = (f32[1,4096]{1,0:T(1,128)S(1)}, f32[1,4096]{1,0:T(1,128)}, u32[]{:S(2)}) copy-start(f32[1,4096]{1,0:T(1,128)} %param.12) | copy-start | bytes 49156
  1.7 25.5 %all-to-all-start = ((bf16[8,48,512]{2,1,0:T(8,128)(2,1)}), bf16[8,48,512]{2,1,0:T(8,128)(2,1)S(1)}, u32[]{:S(2)}, u32[]{:S(2)}) async-start(bf16[8,48,512]{2,1,0:T(8,128)(2,1)} %broadcast_in_dim.80), calls=%async_computation | async-start | bytes 786432 | tf_op jit(solution)/shard_map/all_to_all | solution.py:34
  11.9 15.7 %copy-start.11 = (s32[48,8]{1,0:T(8,128)}, s32[48,8]{1,0:T(8,128)S(1)}, u32[]{:S(2)}) copy-start(s32[48,8]{1,0:T(8,128)S(1)} %copy.53) | copy-start | bytes 4612
  28.1 43.0 %copy-start.2 = (bf16[1,1,4096,128]{3,2,1,0:T(8,128)(2,1)S(1)}, bf16[1,1,4096,128]{3,2,1,0:T(8,128)(2,1)}, u32[]{:S(2)}) copy-start(bf16[1,1,4096,128]{3,2,1,0:T(8,128)(2,1)} %param.16) | copy-start | bytes 3145732
  29.4 43.8 %copy-start.1 = (bf16[1,1,4096,128]{3,2,1,0:T(8,128)(2,1)S(1)}, bf16[1,1,4096,128]{3,2,1,0:T(8,128)(2,1)}, u32[]{:S(2)}) copy-start(bf16[1,1,4096,128]{3,2,1,0:T(8,128)(2,1)} %param.17) | copy-start | bytes 3145732
  78.2 33.6 %all-to-all-start.3 = ((bf16[32,3,4096]{2,1,0:T(4,128)(2,1)}), bf16[32,3,4096]{2,1,0:T(4,128)(2,1)}, u32[]{:S(2)}, u32[]{:S(2)}) async-start(bf16[32,3,4096]{2,1,0:T(4,128)(2,1)} %reshape.267), calls=%async_computation.3 | async-start | bytes 2097152 | tf_op jit(solution)/shard_map/all_to_all | solution.py:129
  114.8 87.7 %all-to-all-start.1 = ((bf16[32,128,384]{2,1,0:T(8,128)(2,1)}), bf16[32,128,384]{2,1,0:T(8,128)(2,1)}, u32[]{:S(2)}, u32[]{:S(2)}) async-start(bf16[32,128,384]{2,1,0:T(8,128)(2,1)} %stack.10), calls=%async_computation.1 | async-start | bytes 6291456 | tf_op jit(solution)/shard_map/all_to_all | solution.py:14
  207.8 52.9 %copy-start.9 = (bf16[3,48,512]{2,1,0:T(8,128)(2,1)S(1)}, bf16[3,48,512]{2,1,0:T(8,128)(2,1)}, u32[]{:S(2)}) copy-start(bf16[3,48,512]{2,1,0:T(8,128)(2,1)} %param.11) | copy-start | bytes 442372
  260.7 2.2 copy-start.17
  260.7 2.2 collective-permute-start
  262.9 0.6 copy-start.3
  264.3 16.8 %all-to-all-start.5 = ((bf16[8,48,512]{2,1,0:T(8,128)(2,1)}), bf16[8,48,512]{2,1,0:T(8,128)(2,1)S(1)}, u32[]{:S(2)}, u32[]{:S(2)}) async-start(bf16[8,48,512]{2,1,0:T(8,128)(2,1)} %broadcast_in_dim.85), calls=%async_computation.5 | async-start | bytes 786432 | tf_op jit(solution)/shard_map/all_to_all | solution.py:34
  281.1 0.7 copy-start.21
  333.1 32.5 %all-to-all-start.7 = ((bf16[32,3,4096]{2,1,0:T(4,128)(2,1)}), bf16[32,3,4096]{2,1,0:T(4,128)(2,1)}, u32[]{:S(2)}, u32[]{:S(2)}) async-start(bf16[32,3,4096]{2,1,0:T(4,128)(2,1)} %reshape.272), calls=%async_computation.7 | async-start | bytes 2097152 | tf_op jit(solution)/shard_map/all_to_all | solution.py:129
  345.9 42.4 %copy-start.4 = (bf16[48,512]{1,0:T(8,128)(2,1)S(1)}, bf16[48,512]{1,0:T(8,128)(2,1)}, u32[]{:S(2)}) copy-start(bf16[48,512]{1,0:T(8,128)(2,1)} %copy-done.3) | copy-start | bytes 147460
  345.9 42.4 %copy-start.18 = (bf16[48,512]{1,0:T(8,128)(2,1)S(1)}, bf16[48,512]{1,0:T(8,128)(2,1)}, u32[]{:S(2)}) copy-start(bf16[48,512]{1,0:T(8,128)(2,1)} %copy-done.17) | copy-start | bytes 147460
  389.0 4.3 copy-start.15
  389.0 2.1 collective-permute-start.1
  391.9 0.6 copy-start.5
  393.3 18.9 %all-to-all-start.9 = ((bf16[8,48,512]{2,1,0:T(8,128)(2,1)}), bf16[8,48,512]{2,1,0:T(8,128)(2,1)S(1)}, u32[]{:S(2)}, u32[]{:S(2)}) async-start(bf16[8,48,512]{2,1,0:T(8,128)(2,1)} %broadcast_in_dim.88), calls=%async_computation.9 | async-start | bytes 786432 | tf_op jit(solution)/shard_map/all_to_all | solution.py:34
  412.2 0.7 copy-start.22
  461.1 33.7 %all-to-all-start.11 = ((bf16[32,3,4096]{2,1,0:T(4,128)(2,1)}), bf16[32,3,4096]{2,1,0:T(4,128)(2,1)}, u32[]{:S(2)}, u32[]{:S(2)}) async-start(bf16[32,3,4096]{2,1,0:T(4,128)(2,1)} %reshape.277), calls=%async_computation.11 | async-start | bytes 2097152 | tf_op jit(solution)/shard_map/all_to_all | solution.py:129
  475.0 42.0 %copy-start.6 = (bf16[48,512]{1,0:T(8,128)(2,1)S(1)}, bf16[48,512]{1,0:T(8,128)(2,1)}, u32[]{:S(2)}) copy-start(bf16[48,512]{1,0:T(8,128)(2,1)} %copy-done.5) | copy-start | bytes 147460
  475.0 42.0 %copy-start.16 = (bf16[48,512]{1,0:T(8,128)(2,1)S(1)}, bf16[48,512]{1,0:T(8,128)(2,1)}, u32[]{:S(2)}) copy-start(bf16[48,512]{1,0:T(8,128)(2,1)} %copy-done.15) | copy-start | bytes 147460
  517.6 4.3 copy-start.19
  517.6 2.1 collective-permute-start.2
  520.5 0.6 copy-start.7
  521.9 19.2 %all-to-all-start.13 = ((bf16[8,48,512]{2,1,0:T(8,128)(2,1)}), bf16[8,48,512]{2,1,0:T(8,128)(2,1)S(1)}, u32[]{:S(2)}, u32[]{:S(2)}) async-start(bf16[8,48,512]{2,1,0:T(8,128)(2,1)} %broadcast_in_dim.91), calls=%async_computation.13 | async-start | bytes 786432 | tf_op jit(solution)/shard_map/all_to_all | solution.py:34
  541.1 0.7 copy-start.23
  585.1 8.6 %copy-start.24 = (f32[48,8]{0,1:T(8,128)S(1)}, f32[48,8]{0,1:T(8,128)}, u32[]{:S(2)}) copy-start(f32[48,8]{0,1:T(8,128)} %get-tuple-element.13) | copy-start | bytes 4612
  585.1 8.7 %copy-start.12 = (s32[48,8]{1,0:T(8,128)S(1)}, s32[48,8]{1,0:T(8,128)}, u32[]{:S(2)}) copy-start(s32[48,8]{1,0:T(8,128)} %copy.65) | copy-start | bytes 4612
  588.2 33.5 %all-to-all-start.15 = ((bf16[32,3,4096]{2,1,0:T(4,128)(2,1)}), bf16[32,3,4096]{2,1,0:T(4,128)(2,1)S(1)}, u32[]{:S(2)}, u32[]{:S(2)}) async-start(bf16[32,3,4096]{2,1,0:T(4,128)(2,1)} %reshape.282), calls=%async_computation.15 | async-start | bytes 2097152 | tf_op jit(solution)/shard_map/all_to_all | solution.py:129
  598.6 43.2 %copy-start.8 = (bf16[48,512]{1,0:T(8,128)(2,1)S(1)}, bf16[48,512]{1,0:T(8,128)(2,1)}, u32[]{:S(2)}) copy-start(bf16[48,512]{1,0:T(8,128)(2,1)} %copy-done.7) | copy-start | bytes 147460
  598.6 43.2 %copy-start.20 = (bf16[48,512]{1,0:T(8,128)(2,1)S(1)}, bf16[48,512]{1,0:T(8,128)(2,1)}, u32[]{:S(2)}) copy-start(bf16[48,512]{1,0:T(8,128)(2,1)} %copy-done.19) | copy-start | bytes 147460
  598.6 43.3 %copy-start.13 = (bf16[1,48,512]{2,1,0:T(8,128)(2,1)S(1)}, bf16[1,48,512]{2,1,0:T(8,128)(2,1)}, u32[]{:S(2)}) copy-start(bf16[1,48,512]{2,1,0:T(8,128)(2,1)} %get-tuple-element.5) | copy-start | bytes 147460
  598.6 43.3 %copy-start.14 = (bf16[1,48,512]{2,1,0:T(8,128)(2,1)S(1)}, bf16[1,48,512]{2,1,0:T(8,128)(2,1)}, u32[]{:S(2)}) copy-start(bf16[1,48,512]{2,1,0:T(8,128)(2,1)} %get-tuple-element.7) | copy-start | bytes 147460
